TPU v7x, 32 devices: a whole 2x2x4 slice. The times are simulated.
32 devices in a mesh: group: 8 (over z, x), tensor: 4 (over y, core).
Axes of the slice: x: 2, y: 2, z: 4, core: 2. Of those that a mesh axis runs over, the one named last changes fastest.
Arguments:
- queries: bfloat16 [64, 64, 5120], P('group', None, 'tensor'), may hold values from -15 to 15
- prefix_keys: bfloat16 [16, 1024, 1024], P('group', None, 'tensor'), may hold values from -200 to 200
- prefix_values: bfloat16 [16, 1024, 1024], P('group', None, 'tensor'), may hold values from -6 to 6
- slot_of_prompt: int32 [16], replicated, may hold values from 0 to 15, as said below
- prompt_of: int32 [64], P('group'), may hold values from 0 to 15, as said below
- lengths: int32 [64], P('group'), may hold values from 1 to 64
Outputs:
- attended: bfloat16 [64, 64, 5120], P('group', 'tensor')
Inputs may be any that keep to these rules, and one draw needn't show every extreme that they name: A permutation: prompt p's keys and values lie in row slot_of_prompt[p] of the prefix arrays, and that row belongs to group index slot_of_prompt[p] // 2. `prompt_of`: of the 8 completions on one group index, at most 2 have prompts cached on any one group index, and on every group index some group index caches the prompts of exactly 2 of them.
All inputs are finite; a program needn't handle non-finite values.
Results may differ from a plain program's by a relative error of at most 0.012.
Values may be sent and summed in bfloat16 or wider, within the bound.
A program may use at most 128 MiB of HBM per device.

v0:
```python
import math

import jax
import jax.numpy as jnp
from jax import lax
from jax.sharding import PartitionSpec as P

HEAD = 128
CAPC = 2


rotary_base = 1000000.0
block_items = 8


def rotary(head_rows, positions):
    half_dim = head_rows.shape[-1] // 2
    frequencies = rotary_base ** (
        -(jnp.arange(half_dim, dtype=jnp.float32) * 2.0 / head_rows.shape[-1])
    )
    angles = positions[:, None] * frequencies[None, :]
    cos_table = jnp.cos(angles)[:, None, :]
    sin_table = jnp.sin(angles)[:, None, :]
    first_half = head_rows[..., :half_dim]
    second_half = head_rows[..., half_dim:]
    return jnp.concatenate(
        [
            first_half * cos_table - second_half * sin_table,
            second_half * cos_table + first_half * sin_table,
        ],
        axis=-1,
    )


def attend_block(query_block, tag_block, cached_keys, cached_values, kv_local):
    slot_items, comp_rows, feature_width = query_block.shape
    cached, prefix_rows, kv_width = cached_keys.shape
    heads_local = feature_width // HEAD
    per_kv = heads_local // kv_local
    selector = (tag_block[:, None] == jnp.arange(cached).astype(jnp.bfloat16)[None, :]).astype(
        jnp.bfloat16
    )
    chosen_keys = jnp.einsum(
        "bc,cpw->bpw", selector, cached_keys, preferred_element_type=jnp.float32
    ).astype(jnp.bfloat16)
    chosen_values = jnp.einsum(
        "bc,cpw->bpw", selector, cached_values, preferred_element_type=jnp.float32
    ).astype(jnp.bfloat16)
    grouped = query_block.reshape(slot_items, comp_rows, kv_local, per_kv, HEAD)
    key_heads = chosen_keys.reshape(slot_items, prefix_rows, kv_local, HEAD)
    value_heads = chosen_values.reshape(slot_items, prefix_rows, kv_local, HEAD)
    scores = jnp.einsum(
        "brkgd,bpkd->bkgrp", grouped, key_heads, preferred_element_type=jnp.float32
    ) * (1.0 / math.sqrt(HEAD))
    peak = jnp.max(scores, axis=-1, keepdims=True)
    weights = jnp.exp(scores - peak)
    denominator = jnp.sum(weights, axis=-1)
    probabilities = weights.astype(jnp.bfloat16)
    weighted = jnp.einsum(
        "bkgrp,bpkd->brkgd", probabilities, value_heads, preferred_element_type=jnp.float32
    )
    attended = weighted / jnp.transpose(denominator, (0, 3, 1, 2))[..., None]
    return attended.astype(jnp.bfloat16).reshape(slot_items, comp_rows, feature_width)


def attend_items(query_items, cache_tags, cached_keys, cached_values, kv_local):
    total_items, comp_rows, feature_width = query_items.shape
    group_size = min(block_items, total_items)
    padding = -total_items % group_size
    padded_items = total_items + padding
    query_blocks = query_items.reshape(
        padded_items // group_size, group_size, comp_rows, feature_width
    )
    tag_blocks = cache_tags.reshape(padded_items // group_size, group_size)

    def compute(pair):
        return attend_block(pair[0], pair[1], cached_keys, cached_values, kv_local)

    results = lax.map(compute, (query_blocks, tag_blocks)).reshape(
        padded_items, comp_rows, feature_width
    )
    return results


def local(queries, prefix_keys, prefix_values, slot_of_prompt, prompt_of, lengths):
    groups = lax.axis_size("group")
    completions_here, comp_rows, feature_width = queries.shape
    cached = prefix_keys.shape[0]
    kv_local = prefix_keys.shape[2] // HEAD
    heads_local = feature_width // HEAD
    positions = (prefix_keys.shape[1] + jnp.arange(comp_rows)).astype(jnp.float32)
    roped = rotary(
        queries.astype(jnp.float32).reshape(completions_here, comp_rows, heads_local, HEAD),
        positions,
    )
    roped = roped.astype(jnp.bfloat16).reshape(completions_here, comp_rows, feature_width)
    cache_rows = slot_of_prompt[prompt_of]
    owner_group = cache_rows // cached
    local_rows = cache_rows % cached
    serial = jnp.arange(completions_here)
    earlier = (owner_group[None, :] == owner_group[:, None]) & (serial[None, :] < serial[:, None])
    arrival = jnp.sum(earlier.astype(jnp.int32), axis=1)
    destination = owner_group * CAPC + arrival
    slot_count = groups * CAPC
    matches = destination[None, :] == jnp.arange(slot_count)[:, None]
    filled = jnp.any(matches, axis=1)
    source_index = jnp.sum(jnp.where(matches, serial[None, :], 0), axis=1)
    outgoing = jnp.where(filled[:, None, None], roped[source_index], jnp.zeros((), jnp.bfloat16))
    outgoing = outgoing.reshape(groups, CAPC, comp_rows, feature_width)
    cache_tags = (
        jnp.where(filled, local_rows[source_index], -1).astype(jnp.bfloat16).reshape(groups, CAPC)
    )
    received = lax.all_to_all(outgoing, "group", split_axis=0, concat_axis=0, tiled=True)
    slot_tags = lax.all_to_all(cache_tags, "group", split_axis=0, concat_axis=0, tiled=True)
    senders, slot_items = slot_tags.shape
    attended = attend_items(
        received.reshape(senders * slot_items, comp_rows, feature_width),
        slot_tags.reshape(senders * slot_items),
        prefix_keys,
        prefix_values,
        kv_local,
    )
    attended = attended.reshape(senders, slot_items, comp_rows, feature_width)
    result = lax.all_to_all(attended, "group", split_axis=0, concat_axis=0, tiled=True)
    flattened = result.reshape(slot_count, result.shape[2], result.shape[3])
    own_rows = flattened[destination]
    row_share = comp_rows // lax.axis_size("tensor")
    attended_rows = lax.all_to_all(own_rows, "tensor", split_axis=1, concat_axis=2, tiled=True)
    row_positions = lax.axis_index("tensor") * row_share + jnp.arange(row_share)
    live_rows = row_positions[None, :] < lengths[:, None]
    return jnp.where(live_rows[:, :, None], attended_rows, jnp.zeros((), jnp.bfloat16))


def solution(mesh):
    placed = (
        P("group", None, "tensor"),
        P("group", None, "tensor"),
        P("group", None, "tensor"),
        P(),
        P("group"),
        P("group"),
    )
    return jax.shard_map(
        local, mesh=mesh, in_specs=placed, out_specs=P("group", "tensor", None), check_vma=False
    )
```

profile of v0, /device:TPU:11, one launch (start us, length us, event | category | flops | bytes accessed | tf_op | source)
XLA Modules:
  0.0 281.5 jit_solution(5476193379303700843)
XLA Ops:
  3.6 5.7 %all-to-all-start = ((bf16[8,1,2]{2,1,0:T(2,128)(2,1)}), bf16[8,1,2]{2,1,0:T(2,128)(2,1)S(1)}, u32[]{:S(2)}, u32[]{:S(2)}) async-start(bf16[8,1,2]{2,1,0:T(2,128)(2,1)} %convert_element_type.61), calls=%async_computation | async-start | bytes 8192 | tf_op jit(solution)/shard_map/all_to_all | solution.py:114
  9.3 4.0 %reshape.272 = f32[8,64,10,128]{3,2,1,0:T(8,128)} reshape(bf16[8,64,1280]{2,1,0:T(8,128)(2,1)} %param.8) | data formatting | bytes 3932160 | tf_op jit(solution)/shard_map/reshape | solution.py:93
  13.5 4.9 %subtract_convert_fusion = (bf16[8,64,10,64]{3,2,1,0:T(8,128)(2,1)S(1)}, bf16[8,64,10,64]{3,2,1,0:T(8,128)(2,1)S(1)}) fusion(f32[8,64,10,128]{3,2,1,0:T(8,128)} %reshape.272, f32[64,64]{1,0:T(8,128)S(1)} %get-tuple-element.91, f32[64,64]{1,0:T(8,128)S(1)} %get-tuple-element.90), kind=kLoop, calls=%fused_computation.35 | loop fusion | flops 2621440 | bytes 3964928 | tf_op jit(solution)/shard_map/convert.1
  20.5 2.2 gather_fusion.2
  22.8 3.5 %broadcast_select_fusion = bf16[8,2,64,1280]{3,2,1,0:T(8,128)(2,1)} fusion(bf16[8,2,64,1280]{3,2,1,0:T(8,128)(2,1)} %bitcast.87, pred[8,2]{1,0:T(8,128)(4,1)S(1)} %broadcast_in_dim.78), kind=kLoop, calls=%fused_computation.36 | loop fusion | flops 1310720 | bytes 5242896 | tf_op jit(solution)/shard_map/jit(_where)/select_n | solution.py:108
  26.3 5.6 %all-to-all-start.1 = ((bf16[8,2,64,1280]{3,2,1,0:T(8,128)(2,1)}), bf16[8,2,64,1280]{3,2,1,0:T(8,128)(2,1)}, u32[]{:S(2)}, u32[]{:S(2)}) async-start(bf16[8,2,64,1280]{3,2,1,0:T(8,128)(2,1)} %broadcast_select_fusion), calls=%async_computation.1 | async-start | bytes 5242880 | tf_op jit(solution)/shard_map/all_to_all | solution.py:113
  31.8 2.0 copy.48
  33.9 2.1 copy.49
  36.1 52.7 %all-to-all-done.1 = bf16[8,2,64,1280]{3,2,1,0:T(8,128)(2,1)} async-done(((bf16[8,2,64,1280]{3,2,1,0:T(8,128)(2,1)}), bf16[8,2,64,1280]{3,2,1,0:T(8,128)(2,1)}, u32[]{:S(2)}, u32[]{:S(2)}) %all-to-all-start.1) | async-done | bytes 2621472 | tf_op jit(solution)/shard_map/all_to_all | solution.py:113
  88.8 100.8 %while.10 = (s32[]{:T(128)}, bf16[2,8,64,1280]{3,2,1,0:T(8,128)(2,1)}, bf16[2,8]{1,0:T(2,128)(2,1)S(1)}, bf16[2,1024,256]{2,0,1:T(2,128)(2,1)}, bf16[2,1024,256]...) while((s32[]{:T(128)}, bf16[2,8,64,1280]{3,2,1,0:T(8,128)(2,1)}, ...), condition=%wide.region_6.7_spmd, body=%wide.region_3.6_spmd.sunk | while | flops 2748569600 | bytes 101814976 | solution.py:79
  88.8 4.3 %convert_bitcast_fusion.4 = bf16[8,1024,2,128,1]{3,0,2,1,4:T(8,128)(2,1)} fusion(bf16[2,1024,256]{2,0,1:T(2,128)(2,1)} %get-tuple-element.153, bf16[8]{0:T(256)(128)(2,1)S(1)} %fusion.47, bf16[2]{0:T(256)(128)(2,1)S(1)} %iota_convert_fusion.2), kind=kOutput, calls=%fused_computation.15.clone.1 | convolution fusion | flops 10485808 | bytes 5242900 | tf_op jit(solution)/shard_map/while/body/eval_jaxpr/bc,cpw->bpw/dot_general | solution.py:43
  93.1 1.4 constant_dynamic-slice_fusion.3
  94.5 1.5 reshape.311
  96.0 12.6 %bitcast_reduce_fusion.2 = (f32[8,2,5,64]{3,2,1,0:T(8,128)S(1)}, f32[8,2,1024,64,5]{2,3,4,1,0:T(8,128)}) fusion(bf16[8,64,2,5,128]{4,3,2,1,0:T(8,128)(2,1)S(1)} %reshape.311, bf16[8,1024,2,128,1]{3,0,2,1,4:T(8,128)(2,1)} %convert_bitcast_fusion.4), kind=kOutput, calls=%fused_computation.5.clone.1 | convolution fusion | flops 1352657920 | bytes 26497024 | tf_op jit(solution)/shard_map/while/body/eval_jaxpr/brkgd,bpkd->bkgrp/dot_general | solution.py:52
  108.6 9.6 %fusion.48 = f32[8,2,5,64]{3,2,1,0:T(8,128)S(1)} fusion(f32[8,2,1024,64,5]{2,3,4,1,0:T(8,128)} %get-tuple-element.133, f32[8,2,5,64]{3,2,1,0:T(8,128)S(1)} %get-tuple-element.134), kind=kLoop, calls=%fused_computation.7.clone.1 | loop fusion | flops 15723520 | bytes 21012480 | tf_op jit(solution)/shard_map/while/body/eval_jaxpr/reduce_sum | solution.py:57
  118.2 3.6 %convert_bitcast_fusion.5 = bf16[8,1024,2,128,1]{3,0,2,1,4:T(8,128)(2,1)} fusion(bf16[2,1024,256]{2,0,1:T(2,128)(2,1)S(1)} %copy-done.2, bf16[8]{0:T(256)(128)(2,1)S(1)} %fusion.47, bf16[2]{0:T(256)(128)(2,1)S(1)} %iota_convert_fusion.2), kind=kOutput, calls=%fused_computation.16.clone.1 | convolution fusion | flops 10485808 | bytes 5242900 | tf_op jit(solution)/shard_map/while/body/eval_jaxpr/bc,cpw->bpw/dot_general | solution.py:46
  121.8 13.8 %fusion.49 = bf16[8,64,2,5,128]{4,1,3,2,0:T(8,128)(2,1)S(1)} fusion(f32[8,2,1024,64,5]{2,3,4,1,0:T(8,128)} %get-tuple-element.133, f32[8,2,5,64]{3,2,1,0:T(8,128)S(1)} %get-tuple-element.134, bf16[8,1024,2,128,1]{3,0,2,1,4:T(8,128)(2,1)} %convert_bitcast_fusion.5, f32[8,64,2,5]{1,3,2,0:T(8,128)S(1)} %bitcast.91), kind=kOutput, calls=%fused_computation.18.clone.1 | convolution fusion | flops 1359216640 | bytes 26517504 | tf_op jit(solution)/shard_map/while/body/eval_jaxpr/bkgrp,bpkd->brkgd/dot_general | solution.py:59
  136.5 1.5 broadcast_in_dim.90
  139.2 4.3 %convert_bitcast_fusion.4 = bf16[8,1024,2,128,1]{3,0,2,1,4:T(8,128)(2,1)} fusion(bf16[2,1024,256]{2,0,1:T(2,128)(2,1)} %get-tuple-element.153, bf16[8]{0:T(256)(128)(2,1)S(1)} %fusion.47, bf16[2]{0:T(256)(128)(2,1)S(1)} %iota_convert_fusion.2), kind=kOutput, calls=%fused_computation.15.clone.1 | convolution fusion | flops 10485808 | bytes 5242900 | tf_op jit(solution)/shard_map/while/body/eval_jaxpr/bc,cpw->bpw/dot_general | solution.py:43
  143.5 1.4 constant_dynamic-slice_fusion.3
  144.9 1.5 reshape.311
  146.4 12.6 %bitcast_reduce_fusion.2 = (f32[8,2,5,64]{3,2,1,0:T(8,128)S(1)}, f32[8,2,1024,64,5]{2,3,4,1,0:T(8,128)}) fusion(bf16[8,64,2,5,128]{4,3,2,1,0:T(8,128)(2,1)S(1)} %reshape.311, bf16[8,1024,2,128,1]{3,0,2,1,4:T(8,128)(2,1)} %convert_bitcast_fusion.4), kind=kOutput, calls=%fused_computation.5.clone.1 | convolution fusion | flops 1352657920 | bytes 26497024 | tf_op jit(solution)/shard_map/while/body/eval_jaxpr/brkgd,bpkd->bkgrp/dot_general | solution.py:52
  159.0 9.6 %fusion.48 = f32[8,2,5,64]{3,2,1,0:T(8,128)S(1)} fusion(f32[8,2,1024,64,5]{2,3,4,1,0:T(8,128)} %get-tuple-element.133, f32[8,2,5,64]{3,2,1,0:T(8,128)S(1)} %get-tuple-element.134), kind=kLoop, calls=%fused_computation.7.clone.1 | loop fusion | flops 15723520 | bytes 21012480 | tf_op jit(solution)/shard_map/while/body/eval_jaxpr/reduce_sum | solution.py:57
  168.6 3.6 %convert_bitcast_fusion.5 = bf16[8,1024,2,128,1]{3,0,2,1,4:T(8,128)(2,1)} fusion(bf16[2,1024,256]{2,0,1:T(2,128)(2,1)S(1)} %copy-done.2, bf16[8]{0:T(256)(128)(2,1)S(1)} %fusion.47, bf16[2]{0:T(256)(128)(2,1)S(1)} %iota_convert_fusion.2), kind=kOutput, calls=%fused_computation.16.clone.1 | convolution fusion | flops 10485808 | bytes 5242900 | tf_op jit(solution)/shard_map/while/body/eval_jaxpr/bc,cpw->bpw/dot_general | solution.py:46
  172.2 13.8 %fusion.49 = bf16[8,64,2,5,128]{4,1,3,2,0:T(8,128)(2,1)S(1)} fusion(f32[8,2,1024,64,5]{2,3,4,1,0:T(8,128)} %get-tuple-element.133, f32[8,2,5,64]{3,2,1,0:T(8,128)S(1)} %get-tuple-element.134, bf16[8,1024,2,128,1]{3,0,2,1,4:T(8,128)(2,1)} %convert_bitcast_fusion.5, f32[8,64,2,5]{1,3,2,0:T(8,128)S(1)} %bitcast.91), kind=kOutput, calls=%fused_computation.18.clone.1 | convolution fusion | flops 1359216640 | bytes 26517504 | tf_op jit(solution)/shard_map/while/body/eval_jaxpr/bkgrp,bpkd->brkgd/dot_general | solution.py:59
  186.9 1.5 broadcast_in_dim.90
  189.6 6.6 %all-to-all-start.2 = ((bf16[8,2,64,1280]{3,2,1,0:T(8,128)(2,1)}), bf16[8,2,64,1280]{3,2,1,0:T(8,128)(2,1)S(1)}, u32[]{:S(2)}, u32[]{:S(2)}) async-start(bf16[8,2,64,1280]{3,2,1,0:T(8,128)(2,1)} %bitcast.90), calls=%async_computation.2 | async-start | bytes 5242880 | tf_op jit(solution)/shard_map/all_to_all | solution.py:124
  196.2 56.9 %all-to-all-done.2 = bf16[8,2,64,1280]{3,2,1,0:T(8,128)(2,1)S(1)} async-done(((bf16[8,2,64,1280]{3,2,1,0:T(8,128)(2,1)}), bf16[8,2,64,1280]{3,2,1,0:T(8,128)(2,1)S(1)}, u32[]{:S(2)}, u32[]{:S(2)}) %all-to-all-start.2) | async-done | bytes 2621472 | tf_op jit(solution)/shard_map/all_to_all | solution.py:124
  253.1 1.7 gather_fusion.3
  254.8 3.1 %copy.50 = bf16[8,64,1280]{2,0,1:T(8,128)(2,1)} copy(bf16[8,64,1280]{2,1,0:T(8,128)(2,1)} %gather_fusion.3) | data formatting | bytes 2621440 | tf_op jit(solution)/shard_map/gather | solution.py:126
  257.9 4.0 %all-to-all-start.3 = ((bf16[8,64,1280]{2,0,1:T(8,128)(2,1)}), bf16[8,64,1280]{2,0,1:T(8,128)(2,1)S(1)}, u32[]{:S(2)}, u32[]{:S(2)}) async-start(bf16[8,64,1280]{2,0,1:T(8,128)(2,1)} %copy.50), calls=%async_computation.3 | async-start | bytes 2621440 | tf_op jit(solution)/shard_map/all_to_all | solution.py:128
  262.0 16.2 %all-to-all-done.3 = bf16[8,64,1280]{2,0,1:T(8,128)(2,1)S(1)} async-done(((bf16[8,64,1280]{2,0,1:T(8,128)(2,1)}), bf16[8,64,1280]{2,0,1:T(8,128)(2,1)S(1)}, u32[]{:S(2)}, u32[]{:S(2)}) %all-to-all-start.3) | async-done | bytes 1310752 | tf_op jit(solution)/shard_map/all_to_all | solution.py:128
  (60 shorter events, 13.7 us)
Async XLA Ops:
  0.0 0.7 copy-start
  1.3 7.9 %copy-start.6 = (s32[8]{0:T(128)}, s32[8]{0:T(128)S(1)}, u32[]{:S(2)}) copy-start(s32[8]{0:T(128)S(1)} %gather_fusion) | copy-start | bytes 100
  1.5 0.6 copy-start.8
  3.6 22.7 %all-to-all-start = ((bf16[8,1,2]{2,1,0:T(2,128)(2,1)}), bf16[8,1,2]{2,1,0:T(2,128)(2,1)S(1)}, u32[]{:S(2)}, u32[]{:S(2)}) async-start(bf16[8,1,2]{2,1,0:T(2,128)(2,1)} %convert_element_type.61), calls=%async_computation | async-start | bytes 8192 | tf_op jit(solution)/shard_map/all_to_all | solution.py:114
  26.3 5.6 %copy-start.3 = (bf16[2,1024,256]{2,1,0:T(8,128)(2,1)S(1)}, bf16[2,1024,256]{2,1,0:T(8,128)(2,1)}, u32[]{:S(2)}) copy-start(bf16[2,1024,256]{2,1,0:T(8,128)(2,1)} %param.10) | copy-start | bytes 3145732
  26.3 7.6 %copy-start.4 = (bf16[2,1024,256]{2,1,0:T(8,128)(2,1)S(1)}, bf16[2,1024,256]{2,1,0:T(8,128)(2,1)}, u32[]{:S(2)}) copy-start(bf16[2,1024,256]{2,1,0:T(8,128)(2,1)} %param.9) | copy-start | bytes 3145732
  26.3 62.5 %all-to-all-start.1 = ((bf16[8,2,64,1280]{3,2,1,0:T(8,128)(2,1)}), bf16[8,2,64,1280]{3,2,1,0:T(8,128)(2,1)}, u32[]{:S(2)}, u32[]{:S(2)}) async-start(bf16[8,2,64,1280]{3,2,1,0:T(8,128)(2,1)} %broadcast_select_fusion), calls=%async_computation.1 | async-start | bytes 5242880 | tf_op jit(solution)/shard_map/all_to_all | solution.py:113
  108.6 9.6 %copy-start.2 = (bf16[2,1024,256]{2,0,1:T(2,128)(2,1)S(1)}, bf16[2,1024,256]{2,0,1:T(2,128)(2,1)}, u32[]{:S(2)}) copy-start(bf16[2,1024,256]{2,0,1:T(2,128)(2,1)} %get-tuple-element.152) | copy-start | bytes 3145732 | tf_op jit(solution)/shard_map/while
  159.0 9.6 %copy-start.2 = (bf16[2,1024,256]{2,0,1:T(2,128)(2,1)S(1)}, bf16[2,1024,256]{2,0,1:T(2,128)(2,1)}, u32[]{:S(2)}) copy-start(bf16[2,1024,256]{2,0,1:T(2,128)(2,1)} %get-tuple-element.152) | copy-start | bytes 3145732 | tf_op jit(solution)/shard_map/while
  189.6 6.6 %copy-start.7 = (s32[8]{0:T(128)S(1)}, s32[8]{0:T(128)}, u32[]{:S(2)}) copy-start(s32[8]{0:T(128)} %copy-done.6) | copy-start | bytes 100
  189.6 6.6 %copy-start.9 = (s32[8]{0:T(128)S(1)}, s32[8]{0:T(128)}, u32[]{:S(2)}) copy-start(s32[8]{0:T(128)} %copy-done.8) | copy-start | bytes 100
  189.6 63.5 %all-to-all-start.2 = ((bf16[8,2,64,1280]{3,2,1,0:T(8,128)(2,1)}), bf16[8,2,64,1280]{3,2,1,0:T(8,128)(2,1)S(1)}, u32[]{:S(2)}, u32[]{:S(2)}) async-start(bf16[8,2,64,1280]{3,2,1,0:T(8,128)(2,1)} %bitcast.90), calls=%async_computation.2 | async-start | bytes 5242880 | tf_op jit(solution)/shard_map/all_to_all | solution.py:124
  254.8 7.1 %copy-start.5 = (s32[8]{0:T(128)S(1)}, s32[8]{0:T(128)}, u32[]{:S(2)}) copy-start(s32[8]{0:T(128)} %param.13) | copy-start | bytes 100
  257.9 20.3 %all-to-all-start.3 = ((bf16[8,64,1280]{2,0,1:T(8,128)(2,1)}), bf16[8,64,1280]{2,0,1:T(8,128)(2,1)S(1)}, u32[]{:S(2)}, u32[]{:S(2)}) async-start(bf16[8,64,1280]{2,0,1:T(8,128)(2,1)} %copy.50), calls=%async_computation.3 | async-start | bytes 2621440 | tf_op jit(solution)/shard_map/all_to_all | solution.py:128
  278.2 3.3 %copy-start.1 = (s32[16]{0:T(128)S(1)}, s32[16]{0:T(128)}, u32[]{:S(2)}) copy-start(s32[16]{0:T(128)} %param.11) | copy-start | bytes 196
where the time goes:
time: 287 us; the launch traced here: 281 us
  waiting for transfers between devices  126 us (44%)
  matrix products  68.6 us (24%)
  local copies, waits for them, and re-layouts  33.6 us (12%)
  other arithmetic  31.4 us (11%)
  starting transfers between devices  21.8 us (8%)
    all_to_all x1, waiting for transfers between devices, local(): lax.all_to_all(attended, 'group', split_axis=0, concat_axis=0, tiled=True)  56.9 us
    all_to_all x1, waiting for transfers between devices, local(): lax.all_to_all(outgoing, 'group', split_axis=0, concat_axis=0, tiled=True)  52.7 us
    dot_general x2, matrix products, attend_block(): jnp.einsum('bkgrp,bpkd->brkgd', probabilities, value_heads, preferred_ele...  27.5 us
    dot_general x2, matrix products, attend_block(): jnp.einsum('brkgd,bpkd->bkgrp', grouped, key_heads, preferred_element_typ...  25.2 us
    reduce_sum x2, other arithmetic, attend_block(): denominator = jnp.sum(weights, axis=-1)  19.1 us
    all_to_all x1, waiting for transfers between devices, local(): lax.all_to_all(own_rows, 'tensor', split_axis=1, concat_axis=2, tiled=True)  16.2 us
    dot_general x2, matrix products, attend_block(): jnp.einsum('bc,cpw->bpw', selector, cached_keys, preferred_element_type=j...  8.63 us
    dot_general x2, matrix products, attend_block(): jnp.einsum('bc,cpw->bpw', selector, cached_values, preferred_element_type...  7.25 us
  transfers between devices with their start and end apart: 4, of which 3 were waited for; matrix products, arithmetic and copies ran while one was open for 8% of the time, Pallas kernels for 0%

commit v1 on v0

v1 whole, which is shorter than its diff:
```python
import functools
import math

import numpy as np

import jax
import jax.numpy as jnp
from jax import lax
from jax.experimental import pallas as pl
from jax.experimental.pallas import tpu as pltpu
from jax.sharding import PartitionSpec as P

HEAD = 128
CAPC = 2
ROTARY_BASE = 1000000.0
TILE = 16
MESH = pl.DeviceIdType.MESH


def rotary_tables(first_position, rows):
    half = HEAD // 2
    frequencies = np.float32(ROTARY_BASE) ** (
        -(np.arange(half, dtype=np.float32) * np.float32(2.0) / np.float32(HEAD))
    )
    positions = (first_position + np.arange(rows)).astype(np.float32)
    angles = (positions[:, None] * frequencies.astype(np.float32)[None, :]).astype(np.float64)
    cos, sin = np.cos(angles), np.sin(angles)
    return (
        np.concatenate([cos, cos], axis=1).astype(np.float32),
        np.concatenate([-sin, sin], axis=1).astype(np.float32),
    )


def kernel(
    groups, lanes,
    source_ref, tag_ref, dest_ref, length_ref,
    q_ref, k_ref, v_ref, cos_ref, sin_ref,
    out_ref,
    q_out, q_in, sel_out, sel_in, res, stage,
    q_send, q_recv, s_send, s_recv, r_send, r_recv,
):
    me, lane = lax.axis_index("group"), lax.axis_index("tensor")
    held, rows, width = q_ref.shape
    cached, prefix, kv_width = k_ref.shape
    share = rows // lanes
    kv_local = kv_width // HEAD
    per_kv = width // HEAD // kv_local
    half = groups // 2
    factor = math.log2(math.e) / math.sqrt(HEAD)

    barrier = pltpu.get_barrier_semaphore()

    def greet(step, carry):
        for turn in range(lanes):
            def send():
                pl.semaphore_signal(
                    barrier, inc=1,
                    device_id=(lax.rem(me + step, groups), lax.rem(lane + turn, lanes)),
                    device_id_type=MESH,
                )
            if turn:
                send()
            else:
                pl.when(step > 0)(send)
        return carry

    lax.fori_loop(0, groups, greet, 0)

    def offset_of(step):
        swing = (step + 1) // 2
        return lax.rem(half + (1 - 2 * lax.rem(step, 2)) * swing + groups, groups)

    def prepare(owner, q_to, sel_to):
        for slot in range(CAPC):
            place = owner * CAPC + slot
            item = source_ref[place]
            tag = tag_ref[place]
            for j in range(cached):
                weight = jnp.where(tag == j, 1.0, 0.0)
                sel_to[owner, slot * cached + j] = jnp.full(
                    (TILE, HEAD), weight, jnp.float32
                ).astype(jnp.bfloat16)
            for head in range(width // HEAD):
                span = slice(head * HEAD, (head + 1) * HEAD)
                x = q_ref[item, :, span].astype(jnp.float32)
                turned = x * cos_ref[...] + pltpu.roll(x, HEAD // 2, 1) * sin_ref[...]
                q_to[owner, slot, :, span] = turned.astype(jnp.bfloat16)

    def q_copy(here, there, device):
        return pltpu.make_async_remote_copy(
            src_ref=q_out.at[here], dst_ref=q_in.at[there],
            send_sem=q_send.at[here], recv_sem=q_recv.at[there],
            device_id=(device, lane), device_id_type=MESH,
        )

    def s_copy(here, there, device):
        return pltpu.make_async_remote_copy(
            src_ref=sel_out.at[here], dst_ref=sel_in.at[there],
            send_sem=s_send.at[here], recv_sem=s_recv.at[there],
            device_id=(device, lane), device_id_type=MESH,
        )

    def r_copy(item, piece, owner, from_lane, device):
        return pltpu.make_async_remote_copy(
            src_ref=res.at[item, :, piece],
            dst_ref=stage.at[
                pl.ds(owner * CAPC, CAPC), :,
                pl.ds(pl.multiple_of(from_lane * width, HEAD), width),
            ],
            send_sem=r_send.at[item, piece], recv_sem=r_recv.at[owner, from_lane],
            device_id=device, device_id_type=MESH,
        )

    def dispatch(step, carry):
        owner = lax.rem(me + offset_of(step), groups)
        prepare(owner, q_out, sel_out)

        @pl.when(step == 0)
        def _():
            pl.semaphore_wait(barrier, groups * lanes - 1)

        s_copy(owner, me, owner).start()
        q_copy(owner, me, owner).start()
        return carry

    lax.fori_loop(0, groups - 1, dispatch, 0)
    prepare(me, q_in, sel_in)

    def attend(source, slot):
        weights = [sel_in[source, slot * cached + j][None] for j in range(cached)]

        def chosen(ref, span):
            total = None
            for j in range(cached):
                part = ref[j, :, span].reshape(prefix // TILE, TILE, HEAD) * weights[j]
                total = part if total is None else total + part
            return total.reshape(prefix, HEAD)

        for kv in range(kv_local):
            span = slice(kv * HEAD, (kv + 1) * HEAD)
            spans = [
                slice((kv * per_kv + g) * HEAD, (kv * per_kv + g + 1) * HEAD)
                for g in range(per_kv)
            ]
            query = jnp.concatenate([q_in[source, slot, :, s] for s in spans], axis=0)
            scores = lax.dot_general(
                query, chosen(k_ref, span), (((1,), (1,)), ((), ())),
                preferred_element_type=jnp.float32,
            )
            peak = jnp.max(scores, axis=-1, keepdims=True)
            weight = jnp.exp2((scores - peak) * factor)
            total = jnp.sum(weight, axis=-1, keepdims=True)
            mixed = jnp.dot(
                weight.astype(jnp.bfloat16), chosen(v_ref, span),
                preferred_element_type=jnp.float32,
            )
            mixed = (mixed / total).astype(jnp.bfloat16)
            for g in range(per_kv):
                res[source, slot, :, :, spans[g]] = mixed[g * rows:(g + 1) * rows].reshape(
                    lanes, share, HEAD
                )

    def work(step, carry):
        source = lax.rem(me + groups - offset_of(lax.rem(step + groups - 1, groups)), groups)

        @pl.when(step > 0)
        def _():
            s_copy(source, source, source).wait_recv()
            q_copy(source, source, source).wait_recv()

        for slot in range(CAPC):
            attend(source, slot)
        for turn in range(1, lanes):
            piece = lax.rem(lane + turn, lanes)
            r_copy(source, piece, me, lane, (source, piece)).start()

        @pl.when(step > 0)
        def _():
            r_copy(source, lane, me, lane, (source, lane)).start()

        @pl.when(step == 0)
        def _():
            stage[
                pl.ds(me * CAPC, CAPC), :,
                pl.ds(pl.multiple_of(lane * width, HEAD), width),
            ] = res[source, :, lane]

        return carry

    lax.fori_loop(0, groups, work, 0)

    def settle(step, carry):
        other = lax.rem(me + step, groups)

        @pl.when(step > 0)
        def _():
            s_copy(other, me, other).wait_send()
            q_copy(other, me, other).wait_send()
            r_copy(other, lane, other, lane, (other, lane)).wait_send()
            r_copy(other, lane, other, lane, (other, lane)).wait_recv()

        for turn in range(1, lanes):
            piece = lax.rem(lane + turn, lanes)
            r_copy(other, piece, other, piece, (other, piece)).wait_send()
            r_copy(other, piece, other, piece, (other, piece)).wait_recv()
        return carry

    lax.fori_loop(0, groups, settle, 0)

    def deliver(item, carry):
        found = stage[dest_ref[item]].astype(jnp.float32)
        position = lane * share + lax.broadcasted_iota(jnp.int32, found.shape, 0)
        out_ref[item] = jnp.where(position < length_ref[item], found, 0.0).astype(jnp.bfloat16)
        return carry

    lax.fori_loop(0, held, deliver, 0)


def local(groups, lanes, queries, prefix_keys, prefix_values, slot_of_prompt, prompt_of, lengths):
    held, rows, width = queries.shape
    cached, prefix, kv_width = prefix_keys.shape
    share = rows // lanes
    cos, sin = rotary_tables(prefix, rows)
    cache_rows = slot_of_prompt[prompt_of]
    owner = cache_rows // cached
    serial = jnp.arange(held)
    earlier = (owner[None, :] == owner[:, None]) & (serial[None, :] < serial[:, None])
    destination = owner * CAPC + jnp.sum(earlier.astype(jnp.int32), axis=1)
    matches = destination[None, :] == jnp.arange(groups * CAPC)[:, None]
    source = jnp.sum(jnp.where(matches, serial[None, :], 0), axis=1)
    tags = jnp.sum(jnp.where(matches, (cache_rows % cached)[None, :], 0), axis=1)
    smem = pl.BlockSpec(memory_space=pltpu.SMEM)
    vmem = pl.BlockSpec(memory_space=pltpu.VMEM)
    dma = pltpu.SemaphoreType.DMA
    bf16 = jnp.bfloat16
    return pl.pallas_call(
        functools.partial(kernel, groups, lanes),
        out_shape=jax.ShapeDtypeStruct((held, share, width * lanes), bf16),
        in_specs=[smem] * 4 + [vmem] * 5,
        out_specs=vmem,
        scratch_shapes=[
            pltpu.VMEM((groups, CAPC, rows, width), bf16),
            pltpu.VMEM((groups, CAPC, rows, width), bf16),
            pltpu.VMEM((groups, CAPC * cached, TILE, HEAD), bf16),
            pltpu.VMEM((groups, CAPC * cached, TILE, HEAD), bf16),
            pltpu.VMEM((groups, CAPC, lanes, share, width), bf16),
            pltpu.VMEM((groups * CAPC, share, width * lanes), bf16),
            dma((groups,)), dma((groups,)),
            dma((groups,)), dma((groups,)),
            dma((groups, lanes)), dma((groups, lanes)),
        ],
        compiler_params=pltpu.CompilerParams(collective_id=0, has_side_effects=True),
        name="routed_prefix_attention",
    )(
        source.astype(jnp.int32), tags.astype(jnp.int32), destination.astype(jnp.int32), lengths,
        queries, prefix_keys, prefix_values, jnp.asarray(cos), jnp.asarray(sin),
    )


def solution(mesh):
    placed = (
        P("group", None, "tensor"),
        P("group", None, "tensor"),
        P("group", None, "tensor"),
        P(),
        P("group"),
        P("group"),
    )
    return jax.shard_map(
        functools.partial(local, mesh.shape["group"], mesh.shape["tensor"]),
        mesh=mesh, in_specs=placed, out_specs=P("group", "tensor", None), check_vma=False,
    )
```

time: 287 us -> 131 us (0.46); the launches traced: 281 us -> 131 us
  Pallas kernels: 0 us -> 126 us
  waiting for transfers between devices: 126 us -> 0 us
  matrix products: 68.6 us -> 0 us
  local copies, waits for them, and re-layouts: 33.6 us -> 3.11 us
  other arithmetic: 31.4 us -> 1.51 us
  starting transfers between devices: 21.8 us -> 0 us
    pallas_call x0 -> x1, Pallas kernels: none -> 126 us  [local(): pl.pallas_call(functools.partial(kernel, groups, lanes), out_shape=jax.Sh...]
    all_to_all x4 -> x0, waiting for transfers between devices: 126 us -> none  [the longest x1 56.9 us: local(): lax.all_to_all(attended, 'group', split_axis=0, concat_axis=0, tiled=True)]
    dot_general x8 -> x0, matrix products: 68.6 us -> none  [the longest x2 27.5 us: attend_block(): jnp.einsum('bkgrp,bpkd->brkgd', probabilities, value_heads, preferred_ele...]
    all_to_all x4 -> x0, starting transfers between devices: 21.8 us -> none  [the longest x1 6.58 us: local(): lax.all_to_all(attended, 'group', split_axis=0, concat_axis=0, tiled=True)]
    reduce_sum x4 -> x2, other arithmetic: 19.4 us -> 0.81 us  [the longest x1 0.63 us: local(): jnp.sum(jnp.where(matches, (cache_rows % cached)[None, :], 0), axis=1)]
    gather x4 -> x0, local copies, waits for them, and re-layouts: 7.67 us -> none  [the longest x2 4.8 us: local(): own_rows = flattened[destination]]
    reshape x3 -> x0, local copies, waits for them, and re-layouts: 6.94 us -> none  [the longest x1 3.95 us: local(): queries.astype(jnp.float32)]
    another operation x1 -> x0, other arithmetic: 4.93 us -> none
  transfers between devices with their start and end apart: 4 -> 0, of which waited for: 3 -> 0; matrix products, arithmetic and copies ran while one was open for 8% -> 0% of each run, Pallas kernels for 0% -> 0%
where the time goes in v1:
time: 131 us
  Pallas kernels  126 us (96%)
  local copies, waits for them, and re-layouts  3.11 us (2%)
  other arithmetic  1.51 us (1%)
    pallas_call x1, Pallas kernels, local(): pl.pallas_call(functools.partial(kernel, groups, lanes), out_shape=jax.Sh...  126 us

profile of v1, /device:TPU:11, one launch (start us, length us, event | category | flops | bytes accessed | tf_op | source)
XLA Modules:
  0.0 131.1 jit_solution(9366149678597761495)
XLA Ops:
  0.0 0.0 copy-start
  0.0 0.7 compare_select_fusion
  0.7 0.0 copy-done
  0.7 0.6 gather_fusion
  1.3 0.2 convert_reduce_fusion
  1.5 0.0 copy-start.1
  1.5 0.6 select_reduce_fusion
  2.2 0.0 copy-done.1
  2.2 126.5 %routed_prefix_attention.1 = bf16[8,16,5120]{2,1,0:T(8,128)(2,1)} custom-call(s32[16]{0:T(128)} %get-tuple-element.6.source_ref, s32[16]{0:T(128)} %get-tuple-element.5.tag_ref, s32[8]{0:T(128)} %copy-done.1, s32[8]{0:T(128)} %length_ref.1, bf16[8,64,1280]{2,1,0:T(8,128)(2,1)} %q_ref.1, bf16[2,1024,256]{2,1,0:T(8,128)(2,1)} %k_ref.1, ...), custom_call_target="tpu_custom_call" | custom-call | tf_op jit(solution)/shard_map/routed_prefix_attention/pallas_call | solution.py:236
  128.7 2.5 %copy.10 = bf16[8,16,5120]{2,1,0:T(8,128)(2,1)} copy(bf16[8,16,5120]{2,1,0:T(8,128)(2,1)} %routed_prefix_attention.1) | data formatting | bytes 2621440
  (3 shorter events, 0.0 us)
Async XLA Ops:
  0.0 0.7 copy-start
  1.5 0.6 copy-start.1
